TPU v7x, 32 devices: a whole 2x2x4 slice. The times are simulated.
32 devices in a mesh: group: 2 (over x), tile: 16 (over z, y, core).
Axes of the slice: x: 2, y: 2, z: 4, core: 2. Of those that a mesh axis runs over, the one named last changes fastest.
Arguments:
- hadamard: int32 [128, 1152], P(None, 'tile'), may hold values from -1 to 1, as said below
- stroke: float32 [2304], P(('group', 'tile')), parts along dimension 0, may hold values from 0.3 to 1
- influence: bfloat16 [3, 2304, 8192], P(None, ('group', 'tile')), parts along dimension 1, may hold values from -0.4375 to 0.4375
- amplitude: float32 [1024, 16, 16], P(('group', 'tile')), parts along dimension 0, may hold values from 0.3 to 1
- aberration: float32 [1024, 16, 16], P(('group', 'tile')), parts along dimension 0, may hold values from -3 to 3
- valid_mask: int32 [1024], P(('group', 'tile')), parts along dimension 0, may hold values from 0 to 1, as said below
Outputs:
- imat: float32 [2304, 2, 512], P(('group', 'tile')), parts along dimension 0
There are 2 independent parts, one for each index of `group`. A program takes and returns all parts, laid end to end along the dimension named above; an argument that names none is the same for every part. Nothing has to cross between parts.
Inputs may be any that keep to these rules, and one draw needn't show every extreme that they name: `hadamard`: each column is one column of a Sylvester-Hadamard matrix whose order is the least power of two not below 1152, restricted to 128 distinct rows of it; different actuators take different columns. `valid_mask`: every pupil tile of 32 subapertures holds at least one valid subaperture.
All inputs are finite; a program needn't handle non-finite values.
Results may differ from a plain program's by a relative error of at most 0.0055.
Values may be sent and summed in bfloat16 or wider, within the bound.
A program may use at most 128 MiB of HBM per device.

v0:
```python
import math
import jax
import jax.numpy as jnp
from jax import lax
from jax.sharding import PartitionSpec as P

PIX = 16
HIGHEST = lax.Precision.HIGHEST


def passed_along(value, axis, steps):
    count = lax.axis_size(axis)
    first, last = (max(0, -steps), min(count, count - steps))
    return lax.ppermute(value, axis, [(source, source + steps) for source in range(first, last)])


def shortened(x):
    return jax.tree.map(lambda a: a.astype(jnp.bfloat16) if a.dtype == jnp.float32 else a, x)


def transform_tables(samples, pixels):
    freqs = jnp.arange(pixels, dtype=jnp.float32) - pixels / 2.0
    places = jnp.arange(samples, dtype=jnp.float32)
    angle = 2.0 * jnp.pi * freqs[:, None] * places[None, :] / (2.0 * samples)
    return (jnp.cos(angle), -jnp.sin(angle))


def kron_tables(samples, pixels):
    table_real, table_imag = transform_tables(samples, pixels)
    kron_real = jnp.kron(table_real, table_real) - jnp.kron(table_imag, table_imag)
    kron_imag = jnp.kron(table_real, table_imag) + jnp.kron(table_imag, table_real)
    upper = jnp.concatenate([kron_real.T, kron_imag.T], axis=1)
    lower = jnp.concatenate([-kron_imag.T, kron_real.T], axis=1)
    transform = jnp.concatenate([upper, lower], axis=0)
    centre = jnp.arange(pixels, dtype=jnp.float32) - (pixels - 1) / 2.0
    along_u = jnp.repeat(centre, pixels)
    along_v = jnp.tile(centre, pixels)
    moments = jnp.stack([jnp.ones_like(along_u), along_u, along_v], axis=1)
    return (transform, moments)


def spot_slopes(phase_map, amplitude, aberration, valid_mask):
    patterns, sub_count, samples = (phase_map.shape[0], phase_map.shape[1], phase_map.shape[2])
    flat = samples * samples
    transform, moments = kron_tables(samples, PIX)
    half = PIX * PIX
    phase_rows = phase_map.reshape(patterns, sub_count, flat)
    amp_rows = amplitude.reshape(sub_count, flat)[None]
    abe_rows = aberration.reshape(sub_count, flat)[None]
    results = []
    for pattern_sign in (1.0, -1.0):
        angles = abe_rows + pattern_sign * phase_rows
        field = jnp.concatenate([amp_rows * jnp.cos(angles), amp_rows * jnp.sin(angles)], axis=2)
        focal = jnp.dot(field.reshape(patterns * sub_count, 2 * flat), transform, precision=HIGHEST)
        intensity = focal[:, :half] * focal[:, :half] + focal[:, half:] * focal[:, half:]
        sums = jnp.dot(intensity, moments, precision=HIGHEST)
        centroid_x = sums[:, 1] / sums[:, 0]
        centroid_y = sums[:, 2] / sums[:, 0]
        results.append(
            jnp.stack([centroid_x, centroid_y], axis=1)
            .reshape(patterns, sub_count, 2)
            .transpose(0, 2, 1)
        )
    weights = valid_mask.astype(jnp.float32)[None, None, :]
    return ((results[0] - results[1]) * 0.5 * weights).astype(jnp.bfloat16)


def shape_term(commands, slab):
    term = jnp.dot(commands, slab, preferred_element_type=jnp.float32).astype(jnp.bfloat16)
    return lax.optimization_barrier(term)


def per_device(hadamard, stroke, influence, amplitude, aberration, valid_mask):
    patterns = hadamard.shape[0]
    sub_count = amplitude.shape[0]
    samples = amplitude.shape[1]
    commands = (stroke[None, :] * hadamard.astype(jnp.float32)).astype(jnp.bfloat16)
    local_term = shape_term(commands, influence[1])
    lower_cmds, lower_slab = passed_along((commands, influence[2]), "tile", 1)
    upper_cmds, upper_slab = passed_along((commands, influence[0]), "tile", -1)
    from_lower = shape_term(lower_cmds, lower_slab)
    from_upper = shape_term(upper_cmds, upper_slab)
    phase_map = (
        local_term.astype(jnp.float32)
        + from_lower.astype(jnp.float32)
        + from_upper.astype(jnp.float32)
    )
    block_rows = math.gcd(patterns, 64)
    blocks = phase_map.reshape(patterns // block_rows, block_rows, sub_count, samples, samples)

    def one_block(pattern_block):
        return spot_slopes(pattern_block, amplitude, aberration, valid_mask)

    slopes = lax.map(one_block, blocks).reshape(patterns, 2, sub_count)
    signs_half = hadamard.astype(jnp.bfloat16)
    summed = jnp.einsum(
        "pa,pcs->acs",
        signs_half,
        lax.all_gather(shortened(slopes), "tile", axis=2, tiled=True),
        preferred_element_type=jnp.float32,
    )
    return summed / (patterns * stroke)[:, None, None]


def solution(mesh):
    placed = (
        P(None, "tile"),
        P(("group", "tile")),
        P(None, ("group", "tile"), None),
        P(("group", "tile"), None, None),
        P(("group", "tile"), None, None),
        P(("group", "tile")),
    )
    return jax.shard_map(
        per_device,
        mesh=mesh,
        in_specs=placed,
        out_specs=P(("group", "tile"), None, None),
        check_vma=False,
    )
```

profile of v0, /device:TPU:0, one launch (start us, length us, event | category | flops | bytes accessed | tf_op | source)
XLA Modules:
  0.0 236.9 jit_solution(5249718799039673560)
XLA Ops:
  0.0 2.8 %slice_bitcast_fusion.1 = (bf16[72,8192]{1,0:T(8,128)(2,1)}, bf16[72,8192]{1,0:T(8,128)(2,1)S(1)}) fusion(bf16[3,72,8192]{2,1,0:T(8,128)(2,1)} %param.10), kind=kLoop, calls=%fused_computation.58 | loop fusion | bytes 4718592 | tf_op jit(solution)/shard_map/squeeze | solution.py:79
  2.8 3.6 %collective-permute-start.1 = (bf16[72,8192]{1,0:T(8,128)(2,1)}, bf16[72,8192]{1,0:T(8,128)(2,1)}, u32[]{:S(2)}, u32[]{:S(2)}) collective-permute-start(bf16[72,8192]{1,0:T(8,128)(2,1)} %get-tuple-element.136), channel_id=1, source_target_pairs={{0,1},{1,2},{2,3},{3,4},{4,5},{5,6},{6,7},{7,8},{8,9},{9,10},{10,1... | collective-permute-start | bytes 3538952 | tf_op jit(solution)/shard_map/ppermute | solution.py:14
  7.8 4.1 %collective-permute-start = (bf16[128,72]{0,1:T(8,128)(2,1)S(1)}, bf16[128,72]{0,1:T(8,128)(2,1)S(1)}, u32[]{:S(2)}, u32[]{:S(2)}) collective-permute-start(bf16[128,72]{0,1:T(8,128)(2,1)S(1)} %multiply_convert_fusion), channel_id=1, source_target_pairs={{0,1},{1,2},{2,3},{3,4},{4,5},{5,6},{6,7},{7,8},{8,9},{9,10},{10,1... | collective-permute-start | bytes 55304 | tf_op jit(solution)/shard_map/ppermute | solution.py:14
  13.2 2.0 convolution_convert_fusion.2
  15.3 2.0 convolution_convert_fusion.1
  17.3 2.0 convolution_convert_fusion
  19.3 2.8 %convert_add_fusion = f32[128,8192]{1,0:T(8,128)} fusion(bf16[128,8192]{1,0:T(8,128)(2,1)S(1)} %convolution_convert_fusion, bf16[128,8192]{1,0:T(8,128)(2,1)S(1)} %convolution_convert_fusion.1, bf16[128,8192]{1,0:T(8,128)(2,1)S(1)} %convolution_convert_fusion.2), kind=kLoop, calls=%fused_computation.55 | loop fusion | flops 5242880 | bytes 10485760 | tf_op jit(solution)/shard_map/add | solution.py:84
  22.1 5.6 %copy.28 = f32[128,8192]{0,1:T(8,128)} copy(f32[128,8192]{1,0:T(8,128)} %convert_add_fusion) | data formatting | bytes 8388608 | tf_op jit(solution)/shard_map/add | solution.py:84
  27.7 9.2 %reshape.211 = f32[2,64,32,16,16]{1,0,4,3,2:T(2,128)} reshape(f32[128,8192]{0,1:T(8,128)} %copy.28) | data formatting | bytes 8388608 | tf_op jit(solution)/shard_map/reshape | solution.py:89
  36.9 159.1 %while.12 = (s32[]{:T(128)}, bf16[2,64,2,32]{1,0,3,2:T(2,128)(2,1)S(1)}, f32[32,16,16]{0,2,1:T(8,128)S(1)}, f32[32,16,16]{0,2,1:T(8,128)S(1)}, f32[2,64,32,16,16...) while((s32[]{:T(128)}, ...), condition=%wide.region_1.2_spmd, body=%wide.region_0.1_spmd.sunk | while | flops 12933627904 | bytes 64969588 | solution.py:94
  36.9 9.7 %constant_dynamic-slice_fusion.2 = f32[1,64,32,16,16]{1,0,4,3,2:T(1,128)} fusion(f32[2,64,32,16,16]{1,0,4,3,2:T(2,128)} %get-tuple-element.223, s32[]{:T(128)} %get-tuple-element.209), kind=kLoop, calls=%fused_computation.46.clone.1 | loop fusion | bytes 4194308 | tf_op jit(solution)/shard_map/while/body/jit(dynamic_index_in_dim)/dynamic_slice | solution.py:94
  46.6 12.3 %copy.40 = f32[1,64,32,16,16]{2,1,4,3,0:T(8,128)} copy(f32[1,64,32,16,16]{1,0,4,3,2:T(1,128)} %constant_dynamic-slice_fusion.2) | data formatting | bytes 4194304 | tf_op jit(solution)/shard_map/while/body/jit(dynamic_index_in_dim)/dynamic_slice | solution.py:94
  58.9 7.5 %reshape.239 = f32[2048,256]{0,1:T(8,128)} reshape(f32[1,64,32,16,16]{2,1,4,3,0:T(8,128)} %copy.40) | data formatting | bytes 4194304 | tf_op jit(solution)/shard_map/while/body/eval_jaxpr/reshape | solution.py:47
  66.4 1.9 copy.41
  68.5 16.6 %bitcast_multiply_fusion.5 = (f32[2048,256]{1,0:T(8,128)}, f32[2048,256]{1,0:T(8,128)}, f32[2048,256]{1,0:T(8,128)}, f32[2048,256]{1,0:T(8,128)}) fusion(f32[2048,256]{1,0:T(8,128)S(1)} %copy.41, f32[32,256]{1,0:T(8,128)S(1)} %copy.42, f32[32,256]{1,0:T(8,128)S(1)} %copy.43), kind=kLoop, calls=%fused_computation.3.clone.1 | loop fusion | flops 3670016 | bytes 10551296 | tf_op jit(solution)/shard_map/while/body/eval_jaxpr/mul | solution.py:53
  85.3 2.0 multiply_add_fusion.2
  87.2 2.4 %add.133 = f32[256,256]{1,0:T(8,128)S(1)} reshape(f32[16,16,16,16]{3,2,1,0:T(8,128)} %get-tuple-element.192) | data formatting | bytes 524288 | tf_op jit(solution)/shard_map/while/body/eval_jaxpr/add | solution.py:31
  90.7 9.8 %fusion.57 = f32[2048,512]{1,0:T(8,128)} fusion(f32[2048,256]{1,0:T(8,128)} %get-tuple-element.193, f32[2048,256]{1,0:T(8,128)} %get-tuple-element.194, f32[256,256]{0,1:T(8,128)S(1)} %bitcast.82, f32[256,256]{0,1:T(8,128)S(1)} %bitcast_negate_fusion.2, f32[256,256]{0,1:T(8,128)S(1)} %bitcast.80), kind=kOutput, calls=%fused_computation.8.clone.1 | convolution fusion | flops 6444285952 | bytes 9175040 | tf_op jit(solution)/shard_map/while/body/eval_jaxpr/dot_general | solution.py:54
  100.7 4.4 %fusion.58 = f32[2048,3]{0,1:T(4,128)S(1)} fusion(f32[2048,512]{1,0:T(8,128)} %fusion.57, f32[256,1]{0,1:T(1,128)S(1)} %tile.19, f32[256,1]{0,1:T(1,128)S(1)} %reshape.240, f32[3]{0:T(128)S(1)} %pad.6.clone.2), kind=kOutput, calls=%fused_computation.16.clone.1 | convolution fusion | flops 20448768 | bytes 4220940 | tf_op jit(solution)/shard_map/while/body/eval_jaxpr/dot_general | solution.py:56
  105.1 8.5 %fusion.55 = f32[2048,512]{1,0:T(8,128)S(1)} fusion(f32[2048,256]{1,0:T(8,128)} %get-tuple-element.187, f32[2048,256]{1,0:T(8,128)S(1)} %copy-done, f32[256,256]{0,1:T(8,128)S(1)} %bitcast.83, f32[256,256]{0,1:T(8,128)S(1)} %bitcast_negate_fusion.2, f32[256,256]{0,1:T(8,128)S(1)} %bitcast.81), kind=kOutput, calls=%fused_computation.4.clone.1 | convolution fusion | flops 6444285952 | bytes 9175040 | tf_op jit(solution)/shard_map/while/body/eval_jaxpr/dot_general | solution.py:54
  113.6 2.0 fusion.56
  116.5 9.7 %constant_dynamic-slice_fusion.2 = f32[1,64,32,16,16]{1,0,4,3,2:T(1,128)} fusion(f32[2,64,32,16,16]{1,0,4,3,2:T(2,128)} %get-tuple-element.223, s32[]{:T(128)} %get-tuple-element.209), kind=kLoop, calls=%fused_computation.46.clone.1 | loop fusion | bytes 4194308 | tf_op jit(solution)/shard_map/while/body/jit(dynamic_index_in_dim)/dynamic_slice | solution.py:94
  126.2 12.3 %copy.40 = f32[1,64,32,16,16]{2,1,4,3,0:T(8,128)} copy(f32[1,64,32,16,16]{1,0,4,3,2:T(1,128)} %constant_dynamic-slice_fusion.2) | data formatting | bytes 4194304 | tf_op jit(solution)/shard_map/while/body/jit(dynamic_index_in_dim)/dynamic_slice | solution.py:94
  138.5 7.5 %reshape.239 = f32[2048,256]{0,1:T(8,128)} reshape(f32[1,64,32,16,16]{2,1,4,3,0:T(8,128)} %copy.40) | data formatting | bytes 4194304 | tf_op jit(solution)/shard_map/while/body/eval_jaxpr/reshape | solution.py:47
  148.1 16.6 %bitcast_multiply_fusion.5 = (f32[2048,256]{1,0:T(8,128)}, f32[2048,256]{1,0:T(8,128)}, f32[2048,256]{1,0:T(8,128)}, f32[2048,256]{1,0:T(8,128)}) fusion(f32[2048,256]{1,0:T(8,128)S(1)} %copy.41, f32[32,256]{1,0:T(8,128)S(1)} %copy.42, f32[32,256]{1,0:T(8,128)S(1)} %copy.43), kind=kLoop, calls=%fused_computation.3.clone.1 | loop fusion | flops 3670016 | bytes 10551296 | tf_op jit(solution)/shard_map/while/body/eval_jaxpr/mul | solution.py:53
  164.8 2.0 multiply_add_fusion.2
  166.8 2.4 %add.133 = f32[256,256]{1,0:T(8,128)S(1)} reshape(f32[16,16,16,16]{3,2,1,0:T(8,128)} %get-tuple-element.192) | data formatting | bytes 524288 | tf_op jit(solution)/shard_map/while/body/eval_jaxpr/add | solution.py:31
  170.2 9.8 %fusion.57 = f32[2048,512]{1,0:T(8,128)} fusion(f32[2048,256]{1,0:T(8,128)} %get-tuple-element.193, f32[2048,256]{1,0:T(8,128)} %get-tuple-element.194, f32[256,256]{0,1:T(8,128)S(1)} %bitcast.82, f32[256,256]{0,1:T(8,128)S(1)} %bitcast_negate_fusion.2, f32[256,256]{0,1:T(8,128)S(1)} %bitcast.80), kind=kOutput, calls=%fused_computation.8.clone.1 | convolution fusion | flops 6444285952 | bytes 9175040 | tf_op jit(solution)/shard_map/while/body/eval_jaxpr/dot_general | solution.py:54
  180.3 4.4 %fusion.58 = f32[2048,3]{0,1:T(4,128)S(1)} fusion(f32[2048,512]{1,0:T(8,128)} %fusion.57, f32[256,1]{0,1:T(1,128)S(1)} %tile.19, f32[256,1]{0,1:T(1,128)S(1)} %reshape.240, f32[3]{0:T(128)S(1)} %pad.6.clone.2), kind=kOutput, calls=%fused_computation.16.clone.1 | convolution fusion | flops 20448768 | bytes 4220940 | tf_op jit(solution)/shard_map/while/body/eval_jaxpr/dot_general | solution.py:56
  184.7 8.5 %fusion.55 = f32[2048,512]{1,0:T(8,128)S(1)} fusion(f32[2048,256]{1,0:T(8,128)} %get-tuple-element.187, f32[2048,256]{1,0:T(8,128)S(1)} %copy-done, f32[256,256]{0,1:T(8,128)S(1)} %bitcast.83, f32[256,256]{0,1:T(8,128)S(1)} %bitcast_negate_fusion.2, f32[256,256]{0,1:T(8,128)S(1)} %bitcast.81), kind=kOutput, calls=%fused_computation.4.clone.1 | convolution fusion | flops 6444285952 | bytes 9175040 | tf_op jit(solution)/shard_map/while/body/eval_jaxpr/dot_general | solution.py:54
  193.2 2.0 fusion.56
  196.1 39.6 %all_gather.3 = bf16[128,2,512]{0,2,1:T(8,128)(2,1)S(1)} all-gather(bf16[128,2,32]{0,2,1:T(8,128)(2,1)S(1)} %reshape.212), channel_id=1, replica_groups=mesh['group'=2,'tile'=16] {'tile'}, dimensions={2}, use_global_device_ids=true | all-gather | bytes 278528 | tf_op jit(solution)/shard_map/all_gather | solution.py:99
  (70 shorter events, 10.4 us)
Async XLA Ops:
  0.0 7.7 %copy-start.3 = (s32[128,72]{0,1:T(8,128)S(1)}, s32[128,72]{0,1:T(8,128)}, u32[]{:S(2)}) copy-start(s32[128,72]{0,1:T(8,128)} %param.8) | copy-start | bytes 110596
  0.0 7.7 %copy-start.4 = (f32[72]{0:T(128)S(1)}, f32[72]{0:T(128)}, u32[]{:S(2)}) copy-start(f32[72]{0:T(128)} %param.9) | copy-start | bytes 868
  2.8 12.4 %copy-start.5 = (s32[32]{0:T(128)S(1)}, s32[32]{0:T(128)}, u32[]{:S(2)}) copy-start(s32[32]{0:T(128)} %param.13) | copy-start | bytes 388
  2.8 12.4 %collective-permute-start.1 = (bf16[72,8192]{1,0:T(8,128)(2,1)}, bf16[72,8192]{1,0:T(8,128)(2,1)}, u32[]{:S(2)}, u32[]{:S(2)}) collective-permute-start(bf16[72,8192]{1,0:T(8,128)(2,1)} %get-tuple-element.136), channel_id=1, source_target_pairs={{0,1},{1,2},{2,3},{3,4},{4,5},{5,6},{6,7},{7,8},{8,9},{9,10},{10,1... | collective-permute-start | bytes 3538952 | tf_op jit(solution)/shard_map/ppermute | solution.py:14
  6.4 10.9 %collective-permute-start.3 = (bf16[72,8192]{1,0:T(8,128)(2,1)S(1)}, bf16[72,8192]{1,0:T(8,128)(2,1)}, u32[]{:S(2)}, u32[]{:S(2)}) collective-permute-start(bf16[72,8192]{1,0:T(8,128)(2,1)S(1)} %get-tuple-element.137), channel_id=1, source_target_pairs={{1,0},{2,1},{3,2},{4,3},{5,4},{6,5},{7,6},{8,7},{9,8},{10,9},{11,1... | collective-permute-start | bytes 3538952 | tf_op jit(solution)/shard_map/ppermute | solution.py:14
  7.8 7.5 %collective-permute-start = (bf16[128,72]{0,1:T(8,128)(2,1)S(1)}, bf16[128,72]{0,1:T(8,128)(2,1)S(1)}, u32[]{:S(2)}, u32[]{:S(2)}) collective-permute-start(bf16[128,72]{0,1:T(8,128)(2,1)S(1)} %multiply_convert_fusion), channel_id=1, source_target_pairs={{0,1},{1,2},{2,3},{3,4},{4,5},{5,6},{6,7},{7,8},{8,9},{9,10},{10,1... | collective-permute-start | bytes 55304 | tf_op jit(solution)/shard_map/ppermute | solution.py:14
  11.9 5.4 %collective-permute-start.2 = (bf16[128,72]{0,1:T(8,128)(2,1)S(1)}, bf16[128,72]{0,1:T(8,128)(2,1)S(1)}, u32[]{:S(2)}, u32[]{:S(2)}) collective-permute-start(bf16[128,72]{0,1:T(8,128)(2,1)S(1)} %multiply_convert_fusion), channel_id=1, source_target_pairs={{1,0},{2,1},{3,2},{4,3},{5,4},{6,5},{7,6},{8,7},{9,8},{10,9},{11,1... | collective-permute-start | bytes 55304 | tf_op jit(solution)/shard_map/ppermute | solution.py:14
  27.7 9.2 %copy-start.1 = (f32[32,16,16]{0,2,1:T(8,128)S(1)}, f32[32,16,16]{0,2,1:T(8,128)}, u32[]{:S(2)}) copy-start(f32[32,16,16]{0,2,1:T(8,128)} %param.11) | copy-start | bytes 98308
  27.7 9.2 %copy-start.2 = (f32[32,16,16]{0,2,1:T(8,128)S(1)}, f32[32,16,16]{0,2,1:T(8,128)}, u32[]{:S(2)}) copy-start(f32[32,16,16]{0,2,1:T(8,128)} %param.12) | copy-start | bytes 98308
  100.5 4.7 %copy-start = (f32[2048,256]{1,0:T(8,128)S(1)}, f32[2048,256]{1,0:T(8,128)}, u32[]{:S(2)}) copy-start(f32[2048,256]{1,0:T(8,128)} %get-tuple-element.188) | copy-start | bytes 6291460 | tf_op jit(solution)/shard_map/while
  180.0 4.7 %copy-start = (f32[2048,256]{1,0:T(8,128)S(1)}, f32[2048,256]{1,0:T(8,128)}, u32[]{:S(2)}) copy-start(f32[2048,256]{1,0:T(8,128)} %get-tuple-element.188) | copy-start | bytes 6291460 | tf_op jit(solution)/shard_map/while
where the time goes:
time: 238 us; the launch traced here: 237 us
  local copies, waits for them, and re-layouts  90.3 us (38%)
  matrix products  55.7 us (23%)
  other arithmetic  40.7 us (17%)
  blocking collectives  39.6 us (17%)
  starting transfers between devices  10.3 us (4%)
    dynamic_slice x4, local copies, waits for them, and re-layouts, per_device(): slopes = lax.map(one_block, blocks).reshape(patterns, 2, sub_count)  44.1 us
    all_gather x1, blocking collectives, per_device(): lax.all_gather(shortened(slopes), 'tile', axis=2, tiled=True)  39.6 us
    dot_general x4, matrix products, spot_slopes(): jnp.dot(field.reshape(patterns * sub_count, 2 * flat), transform, precisi...  36.6 us
    mul x2, other arithmetic, spot_slopes(): amp_rows * jnp.cos(angles)  33.3 us
    reshape x4, local copies, waits for them, and re-layouts, spot_slopes(): phase_rows = phase_map.reshape(patterns, sub_count, flat)  18.8 us
    dot_general x4, matrix products, spot_slopes(): sums = jnp.dot(intensity, moments, precision=HIGHEST)  12.9 us
    ppermute x4, starting transfers between devices, passed_along(): lax.ppermute(value, axis, [(source, source + steps) for source in range(f...  10.3 us
    reshape x1, local copies, waits for them, and re-layouts, per_device(): phase_map.reshape(patterns // block_rows, block_rows, sub_count, samples,...  9.2 us
  transfers between devices with their start and end apart: 4, of which 0 were waited for; matrix products, arithmetic and copies ran while one was open for 2% of the time, Pallas kernels for 0%

commit v1 on v0

--- a/solution.py
+++ b/solution.py
@@ -6,6 +6,18 @@
 
 PIX = 16
 HIGHEST = lax.Precision.HIGHEST
+
+
+def gather_by_bits(x, axis, dim):
+    ways, here = (lax.axis_size(axis), lax.axis_index(axis))
+    grown, reach = (x, 1)
+    while reach < ways:
+        theirs = lax.ppermute(grown, axis, [(d, d ^ reach) for d in range(ways)])
+        mine_first = jnp.concatenate([grown, theirs], axis=dim)
+        theirs_first = jnp.concatenate([theirs, grown], axis=dim)
+        grown = jnp.where(here & reach == 0, mine_first, theirs_first)
+        reach = 2 * reach
+    return grown
 
 
 def passed_along(value, axis, steps):
@@ -96,7 +108,7 @@
     summed = jnp.einsum(
         "pa,pcs->acs",
         signs_half,
-        lax.all_gather(shortened(slopes), "tile", axis=2, tiled=True),
+        gather_by_bits(shortened(slopes), "tile", 2),
         preferred_element_type=jnp.float32,
     )
     return summed / (patterns * stroke)[:, None, None]

time: 238 us -> 235 us (0.987)
  blocking collectives: 39.6 us -> 0 us
  starting transfers between devices: 10.3 us -> 36.5 us
  waiting for transfers between devices: 0.01 us -> 10.1 us
    all_gather x1 -> x0, blocking collectives: 39.6 us -> none  [per_device(): lax.all_gather(shortened(slopes), 'tile', axis=2, tiled=True)]
    ppermute x0 -> x4, starting transfers between devices: none -> 26.2 us  [gather_by_bits(): theirs = lax.ppermute(grown, axis, [(d, d ^ reach) for d in range(ways)])]
    ppermute x0 -> x4, waiting for transfers between devices: none -> 10.1 us  [gather_by_bits(): theirs = lax.ppermute(grown, axis, [(d, d ^ reach) for d in range(ways)])]
  transfers between devices with their start and end apart: 4 -> 8, of which waited for: 0 -> 4; matrix products, arithmetic and copies ran while one was open for 2% -> 2% of each run, Pallas kernels for 0% -> 0%
where the time goes in v1:
time: 235 us; the launch traced here: 234 us
  local copies, waits for them, and re-layouts  90.3 us (38%)
  matrix products  55.8 us (24%)
  other arithmetic  40.8 us (17%)
  starting transfers between devices  36.5 us (16%)
  waiting for transfers between devices  10.1 us (4%)
    dynamic_slice x4, local copies, waits for them, and re-layouts, per_device(): slopes = lax.map(one_block, blocks).reshape(patterns, 2, sub_count)  44.1 us
    dot_general x4, matrix products, spot_slopes(): jnp.dot(field.reshape(patterns * sub_count, 2 * flat), transform, precisi...  36.6 us
    mul x2, other arithmetic, spot_slopes(): amp_rows * jnp.cos(angles)  33.2 us
    ppermute x4, starting transfers between devices, gather_by_bits(): theirs = lax.ppermute(grown, axis, [(d, d ^ reach) for d in range(ways)])  26.2 us
    reshape x4, local copies, waits for them, and re-layouts, spot_slopes(): phase_rows = phase_map.reshape(patterns, sub_count, flat)  18.8 us
    dot_general x4, matrix products, spot_slopes(): sums = jnp.dot(intensity, moments, precision=HIGHEST)  12.9 us
    ppermute x4, starting transfers between devices, passed_along(): lax.ppermute(value, axis, [(source, source + steps) for source in range(f...  10.3 us
    ppermute x4, waiting for transfers between devices, gather_by_bits(): theirs = lax.ppermute(grown, axis, [(d, d ^ reach) for d in range(ways)])  10.1 us
  transfers between devices with their start and end apart: 8, of which 4 were waited for; matrix products, arithmetic and copies ran while one was open for 2% of the time, Pallas kernels for 0%

profile of v1, /device:TPU:0, one launch (start us, length us, event | category | flops | bytes accessed | tf_op | source)
XLA Modules:
  0.0 233.8 jit_solution(15763440504330136849)
XLA Ops:
  0.0 2.9 %slice_bitcast_fusion.1 = (bf16[72,8192]{1,0:T(8,128)(2,1)}, bf16[72,8192]{1,0:T(8,128)(2,1)S(1)}) fusion(bf16[3,72,8192]{2,1,0:T(8,128)(2,1)} %param.10), kind=kLoop, calls=%fused_computation.58 | loop fusion | bytes 4718592 | tf_op jit(solution)/shard_map/squeeze | solution.py:91
  2.9 3.6 %collective-permute-start.1 = (bf16[72,8192]{1,0:T(8,128)(2,1)}, bf16[72,8192]{1,0:T(8,128)(2,1)}, u32[]{:S(2)}, u32[]{:S(2)}) collective-permute-start(bf16[72,8192]{1,0:T(8,128)(2,1)} %get-tuple-element.136), channel_id=1, source_target_pairs={{0,1},{1,2},{2,3},{3,4},{4,5},{5,6},{6,7},{7,8},{8,9},{9,10},{10,1... | collective-permute-start | bytes 3538952 | tf_op jit(solution)/shard_map/ppermute | solution.py:26
  7.8 4.1 %collective-permute-start = (bf16[128,72]{0,1:T(8,128)(2,1)S(1)}, bf16[128,72]{0,1:T(8,128)(2,1)S(1)}, u32[]{:S(2)}, u32[]{:S(2)}) collective-permute-start(bf16[128,72]{0,1:T(8,128)(2,1)S(1)} %multiply_convert_fusion), channel_id=1, source_target_pairs={{0,1},{1,2},{2,3},{3,4},{4,5},{5,6},{6,7},{7,8},{8,9},{9,10},{10,1... | collective-permute-start | bytes 55304 | tf_op jit(solution)/shard_map/ppermute | solution.py:26
  13.2 2.0 convolution_convert_fusion.2
  19.3 2.8 %convert_add_fusion = f32[128,8192]{1,0:T(8,128)} fusion(bf16[128,8192]{1,0:T(8,128)(2,1)S(1)} %convolution_convert_fusion, bf16[128,8192]{1,0:T(8,128)(2,1)S(1)} %convolution_convert_fusion.1, bf16[128,8192]{1,0:T(8,128)(2,1)S(1)} %convolution_convert_fusion.2), kind=kLoop, calls=%fused_computation.55 | loop fusion | flops 5242880 | bytes 10485760 | tf_op jit(solution)/shard_map/add | solution.py:96
  22.1 5.6 %copy.29 = f32[128,8192]{0,1:T(8,128)} copy(f32[128,8192]{1,0:T(8,128)} %convert_add_fusion) | data formatting | bytes 8388608 | tf_op jit(solution)/shard_map/add | solution.py:96
  27.7 9.2 %reshape.211 = f32[2,64,32,16,16]{1,0,4,3,2:T(2,128)} reshape(f32[128,8192]{0,1:T(8,128)} %copy.29) | data formatting | bytes 8388608 | tf_op jit(solution)/shard_map/reshape | solution.py:101
  36.9 159.1 %while.12 = (s32[]{:T(128)}, bf16[2,64,2,32]{1,0,3,2:T(2,128)(2,1)S(1)}, f32[32,16,16]{0,2,1:T(8,128)S(1)}, f32[32,16,16]{0,2,1:T(8,128)S(1)}, f32[2,64,32,16,16...) while((s32[]{:T(128)}, ...), condition=%wide.region_1.2_spmd, body=%wide.region_0.1_spmd.sunk | while | flops 12933627904 | bytes 64969588 | solution.py:106
  36.9 9.7 %constant_dynamic-slice_fusion.2 = f32[1,64,32,16,16]{1,0,4,3,2:T(1,128)} fusion(f32[2,64,32,16,16]{1,0,4,3,2:T(2,128)} %get-tuple-element.223, s32[]{:T(128)} %get-tuple-element.209), kind=kLoop, calls=%fused_computation.46.clone.1 | loop fusion | bytes 4194308 | tf_op jit(solution)/shard_map/while/body/jit(dynamic_index_in_dim)/dynamic_slice | solution.py:106
  46.7 12.3 %copy.43 = f32[1,64,32,16,16]{2,1,4,3,0:T(8,128)} copy(f32[1,64,32,16,16]{1,0,4,3,2:T(1,128)} %constant_dynamic-slice_fusion.2) | data formatting | bytes 4194304 | tf_op jit(solution)/shard_map/while/body/jit(dynamic_index_in_dim)/dynamic_slice | solution.py:106
  59.0 7.5 %reshape.239 = f32[2048,256]{0,1:T(8,128)} reshape(f32[1,64,32,16,16]{2,1,4,3,0:T(8,128)} %copy.43) | data formatting | bytes 4194304 | tf_op jit(solution)/shard_map/while/body/eval_jaxpr/reshape | solution.py:59
  68.5 16.6 %bitcast_multiply_fusion.5 = (f32[2048,256]{1,0:T(8,128)}, f32[2048,256]{1,0:T(8,128)}, f32[2048,256]{1,0:T(8,128)}, f32[2048,256]{1,0:T(8,128)}) fusion(f32[2048,256]{1,0:T(8,128)S(1)} %copy.44, f32[32,256]{1,0:T(8,128)S(1)} %copy.45, f32[32,256]{1,0:T(8,128)S(1)} %copy.46), kind=kLoop, calls=%fused_computation.3.clone.1 | loop fusion | flops 3670016 | bytes 10551296 | tf_op jit(solution)/shard_map/while/body/eval_jaxpr/mul | solution.py:65
  87.3 2.4 %add.133 = f32[256,256]{1,0:T(8,128)S(1)} reshape(f32[16,16,16,16]{3,2,1,0:T(8,128)} %get-tuple-element.192) | data formatting | bytes 524288 | tf_op jit(solution)/shard_map/while/body/eval_jaxpr/add | solution.py:43
  90.7 9.8 %fusion.63 = f32[2048,512]{1,0:T(8,128)} fusion(f32[2048,256]{1,0:T(8,128)} %get-tuple-element.193, f32[2048,256]{1,0:T(8,128)} %get-tuple-element.194, f32[256,256]{0,1:T(8,128)S(1)} %bitcast.81, f32[256,256]{0,1:T(8,128)S(1)} %bitcast_negate_fusion.2, f32[256,256]{0,1:T(8,128)S(1)} %bitcast.79), kind=kOutput, calls=%fused_computation.8.clone.1 | convolution fusion | flops 6444285952 | bytes 9175040 | tf_op jit(solution)/shard_map/while/body/eval_jaxpr/dot_general | solution.py:66
  100.8 4.4 %fusion.64 = f32[2048,3]{0,1:T(4,128)S(1)} fusion(f32[2048,512]{1,0:T(8,128)} %fusion.63, f32[256,1]{0,1:T(1,128)S(1)} %tile.19, f32[256,1]{0,1:T(1,128)S(1)} %reshape.240, f32[3]{0:T(128)S(1)} %pad.6.clone.2), kind=kOutput, calls=%fused_computation.16.clone.1 | convolution fusion | flops 20448768 | bytes 4220940 | tf_op jit(solution)/shard_map/while/body/eval_jaxpr/dot_general | solution.py:68
  105.1 8.5 %fusion.61 = f32[2048,512]{1,0:T(8,128)S(1)} fusion(f32[2048,256]{1,0:T(8,128)} %get-tuple-element.187, f32[2048,256]{1,0:T(8,128)S(1)} %copy-done, f32[256,256]{0,1:T(8,128)S(1)} %bitcast.82, f32[256,256]{0,1:T(8,128)S(1)} %bitcast_negate_fusion.2, f32[256,256]{0,1:T(8,128)S(1)} %bitcast.80), kind=kOutput, calls=%fused_computation.4.clone.1 | convolution fusion | flops 6444285952 | bytes 9175040 | tf_op jit(solution)/shard_map/while/body/eval_jaxpr/dot_general | solution.py:66
  113.6 2.0 fusion.62
  116.5 9.7 %constant_dynamic-slice_fusion.2 = f32[1,64,32,16,16]{1,0,4,3,2:T(1,128)} fusion(f32[2,64,32,16,16]{1,0,4,3,2:T(2,128)} %get-tuple-element.223, s32[]{:T(128)} %get-tuple-element.209), kind=kLoop, calls=%fused_computation.46.clone.1 | loop fusion | bytes 4194308 | tf_op jit(solution)/shard_map/while/body/jit(dynamic_index_in_dim)/dynamic_slice | solution.py:106
  126.2 12.3 %copy.43 = f32[1,64,32,16,16]{2,1,4,3,0:T(8,128)} copy(f32[1,64,32,16,16]{1,0,4,3,2:T(1,128)} %constant_dynamic-slice_fusion.2) | data formatting | bytes 4194304 | tf_op jit(solution)/shard_map/while/body/jit(dynamic_index_in_dim)/dynamic_slice | solution.py:106
  138.5 7.5 %reshape.239 = f32[2048,256]{0,1:T(8,128)} reshape(f32[1,64,32,16,16]{2,1,4,3,0:T(8,128)} %copy.43) | data formatting | bytes 4194304 | tf_op jit(solution)/shard_map/while/body/eval_jaxpr/reshape | solution.py:59
  148.1 16.6 %bitcast_multiply_fusion.5 = (f32[2048,256]{1,0:T(8,128)}, f32[2048,256]{1,0:T(8,128)}, f32[2048,256]{1,0:T(8,128)}, f32[2048,256]{1,0:T(8,128)}) fusion(f32[2048,256]{1,0:T(8,128)S(1)} %copy.44, f32[32,256]{1,0:T(8,128)S(1)} %copy.45, f32[32,256]{1,0:T(8,128)S(1)} %copy.46), kind=kLoop, calls=%fused_computation.3.clone.1 | loop fusion | flops 3670016 | bytes 10551296 | tf_op jit(solution)/shard_map/while/body/eval_jaxpr/mul | solution.py:65
  164.8 2.0 multiply_add_fusion.2
  166.8 2.4 %add.133 = f32[256,256]{1,0:T(8,128)S(1)} reshape(f32[16,16,16,16]{3,2,1,0:T(8,128)} %get-tuple-element.192) | data formatting | bytes 524288 | tf_op jit(solution)/shard_map/while/body/eval_jaxpr/add | solution.py:43
  170.2 9.8 %fusion.63 = f32[2048,512]{1,0:T(8,128)} fusion(f32[2048,256]{1,0:T(8,128)} %get-tuple-element.193, f32[2048,256]{1,0:T(8,128)} %get-tuple-element.194, f32[256,256]{0,1:T(8,128)S(1)} %bitcast.81, f32[256,256]{0,1:T(8,128)S(1)} %bitcast_negate_fusion.2, f32[256,256]{0,1:T(8,128)S(1)} %bitcast.79), kind=kOutput, calls=%fused_computation.8.clone.1 | convolution fusion | flops 6444285952 | bytes 9175040 | tf_op jit(solution)/shard_map/while/body/eval_jaxpr/dot_general | solution.py:66
  180.3 4.4 %fusion.64 = f32[2048,3]{0,1:T(4,128)S(1)} fusion(f32[2048,512]{1,0:T(8,128)} %fusion.63, f32[256,1]{0,1:T(1,128)S(1)} %tile.19, f32[256,1]{0,1:T(1,128)S(1)} %reshape.240, f32[3]{0:T(128)S(1)} %pad.6.clone.2), kind=kOutput, calls=%fused_computation.16.clone.1 | convolution fusion | flops 20448768 | bytes 4220940 | tf_op jit(solution)/shard_map/while/body/eval_jaxpr/dot_general | solution.py:68
  184.7 8.5 %fusion.61 = f32[2048,512]{1,0:T(8,128)S(1)} fusion(f32[2048,256]{1,0:T(8,128)} %get-tuple-element.187, f32[2048,256]{1,0:T(8,128)S(1)} %copy-done, f32[256,256]{0,1:T(8,128)S(1)} %bitcast.82, f32[256,256]{0,1:T(8,128)S(1)} %bitcast_negate_fusion.2, f32[256,256]{0,1:T(8,128)S(1)} %bitcast.80), kind=kOutput, calls=%fused_computation.4.clone.1 | convolution fusion | flops 6444285952 | bytes 9175040 | tf_op jit(solution)/shard_map/while/body/eval_jaxpr/dot_general | solution.py:66
  193.2 2.0 fusion.62
  196.1 19.1 %collective-permute-start.4 = (bf16[128,2,32]{0,2,1:T(8,128)(2,1)S(1)}, bf16[128,2,32]{0,2,1:T(8,128)(2,1)S(1)}, u32[]{:S(2)}, u32[]{:S(2)}) collective-permute-start(bf16[128,2,32]{0,2,1:T(8,128)(2,1)S(1)} %reshape.212), channel_id=1, source_target_pairs={{0,1},{1,0},{2,3},{3,2},{4,5},{5,4},{6,7},{7,6},{8,9},{9,8},{10,11... | collective-permute-start | bytes 49160 | tf_op jit(solution)/shard_map/ppermute | solution.py:15
  216.1 2.8 %collective-permute-start.5 = (bf16[128,2,64]{0,2,1:T(8,128)(2,1)S(1)}, bf16[128,2,64]{0,2,1:T(8,128)(2,1)S(1)}, u32[]{:S(2)}, u32[]{:S(2)}) collective-permute-start(bf16[128,2,64]{0,2,1:T(8,128)(2,1)S(1)} %maximum_select_fusion.4), channel_id=1, source_target_pairs={{0,2},{1,3},{2,0},{3,1},{4,6},{5,7},{6,4},{7,5},{8,10},{9,11},{10,... | collective-permute-start | bytes 98312 | tf_op jit(solution)/shard_map/ppermute | solution.py:15
  222.5 2.7 %collective-permute-done.6 = bf16[128,2,128]{0,2,1:T(8,128)(2,1)S(1)} collective-permute-done((bf16[128,2,128]{0,2,1:T(8,128)(2,1)S(1)}, bf16[128,2,128]{0,2,1:T(8,128)(2,1)S(1)}, u32[]{:S(2)}, u32[]{:S(2)}) %collective-permute-start.6) | collective-permute-done | bytes 65568 | tf_op jit(solution)/shard_map/ppermute | solution.py:15
  225.2 2.7 %collective-permute-start.7 = (bf16[128,2,256]{0,2,1:T(8,128)(2,1)S(1)}, bf16[128,2,256]{0,2,1:T(8,128)(2,1)S(1)}, u32[]{:S(2)}, u32[]{:S(2)}) collective-permute-start(bf16[128,2,256]{0,2,1:T(8,128)(2,1)S(1)} %maximum_select_fusion.2), channel_id=1, source_target_pairs={{0,8},{1,9},{2,10},{3,11},{4,12},{5,13},{6,14},{7,15},{8,0},{9,1},... | collective-permute-start | bytes 393224 | tf_op jit(solution)/shard_map/ppermute | solution.py:15
  227.9 4.7 %collective-permute-done.7 = bf16[128,2,256]{0,2,1:T(8,128)(2,1)S(1)} collective-permute-done((bf16[128,2,256]{0,2,1:T(8,128)(2,1)S(1)}, bf16[128,2,256]{0,2,1:T(8,128)(2,1)S(1)}, u32[]{:S(2)}, u32[]{:S(2)}) %collective-permute-start.7) | collective-permute-done | bytes 131104 | tf_op jit(solution)/shard_map/ppermute | solution.py:15
  (80 shorter events, 22.8 us)
Async XLA Ops:
  0.0 7.7 %copy-start.3 = (s32[128,72]{0,1:T(8,128)S(1)}, s32[128,72]{0,1:T(8,128)}, u32[]{:S(2)}) copy-start(s32[128,72]{0,1:T(8,128)} %param.8) | copy-start | bytes 110596
  0.0 7.7 %copy-start.4 = (f32[72]{0:T(128)S(1)}, f32[72]{0:T(128)}, u32[]{:S(2)}) copy-start(f32[72]{0:T(128)} %param.9) | copy-start | bytes 868
  2.9 12.4 %copy-start.5 = (s32[32]{0:T(128)S(1)}, s32[32]{0:T(128)}, u32[]{:S(2)}) copy-start(s32[32]{0:T(128)} %param.13) | copy-start | bytes 388
  2.9 12.4 %collective-permute-start.1 = (bf16[72,8192]{1,0:T(8,128)(2,1)}, bf16[72,8192]{1,0:T(8,128)(2,1)}, u32[]{:S(2)}, u32[]{:S(2)}) collective-permute-start(bf16[72,8192]{1,0:T(8,128)(2,1)} %get-tuple-element.136), channel_id=1, source_target_pairs={{0,1},{1,2},{2,3},{3,4},{4,5},{5,6},{6,7},{7,8},{8,9},{9,10},{10,1... | collective-permute-start | bytes 3538952 | tf_op jit(solution)/shard_map/ppermute | solution.py:26
  6.4 10.9 %collective-permute-start.3 = (bf16[72,8192]{1,0:T(8,128)(2,1)S(1)}, bf16[72,8192]{1,0:T(8,128)(2,1)}, u32[]{:S(2)}, u32[]{:S(2)}) collective-permute-start(bf16[72,8192]{1,0:T(8,128)(2,1)S(1)} %get-tuple-element.137), channel_id=1, source_target_pairs={{1,0},{2,1},{3,2},{4,3},{5,4},{6,5},{7,6},{8,7},{9,8},{10,9},{11,1... | collective-permute-start | bytes 3538952 | tf_op jit(solution)/shard_map/ppermute | solution.py:26
  7.8 7.5 %collective-permute-start = (bf16[128,72]{0,1:T(8,128)(2,1)S(1)}, bf16[128,72]{0,1:T(8,128)(2,1)S(1)}, u32[]{:S(2)}, u32[]{:S(2)}) collective-permute-start(bf16[128,72]{0,1:T(8,128)(2,1)S(1)} %multiply_convert_fusion), channel_id=1, source_target_pairs={{0,1},{1,2},{2,3},{3,4},{4,5},{5,6},{6,7},{7,8},{8,9},{9,10},{10,1... | collective-permute-start | bytes 55304 | tf_op jit(solution)/shard_map/ppermute | solution.py:26
  11.9 5.4 %collective-permute-start.2 = (bf16[128,72]{0,1:T(8,128)(2,1)S(1)}, bf16[128,72]{0,1:T(8,128)(2,1)S(1)}, u32[]{:S(2)}, u32[]{:S(2)}) collective-permute-start(bf16[128,72]{0,1:T(8,128)(2,1)S(1)} %multiply_convert_fusion), channel_id=1, source_target_pairs={{1,0},{2,1},{3,2},{4,3},{5,4},{6,5},{7,6},{8,7},{9,8},{10,9},{11,1... | collective-permute-start | bytes 55304 | tf_op jit(solution)/shard_map/ppermute | solution.py:26
  27.7 9.2 %copy-start.1 = (f32[32,16,16]{0,2,1:T(8,128)S(1)}, f32[32,16,16]{0,2,1:T(8,128)}, u32[]{:S(2)}) copy-start(f32[32,16,16]{0,2,1:T(8,128)} %param.11) | copy-start | bytes 98308
  27.7 9.2 %copy-start.2 = (f32[32,16,16]{0,2,1:T(8,128)S(1)}, f32[32,16,16]{0,2,1:T(8,128)}, u32[]{:S(2)}) copy-start(f32[32,16,16]{0,2,1:T(8,128)} %param.12) | copy-start | bytes 98308
  100.5 4.7 %copy-start = (f32[2048,256]{1,0:T(8,128)S(1)}, f32[2048,256]{1,0:T(8,128)}, u32[]{:S(2)}) copy-start(f32[2048,256]{1,0:T(8,128)} %get-tuple-element.188) | copy-start | bytes 6291460 | tf_op jit(solution)/shard_map/while
  180.1 4.7 %copy-start = (f32[2048,256]{1,0:T(8,128)S(1)}, f32[2048,256]{1,0:T(8,128)}, u32[]{:S(2)}) copy-start(f32[2048,256]{1,0:T(8,128)} %get-tuple-element.188) | copy-start | bytes 6291460 | tf_op jit(solution)/shard_map/while
  196.1 20.0 %collective-permute-start.4 = (bf16[128,2,32]{0,2,1:T(8,128)(2,1)S(1)}, bf16[128,2,32]{0,2,1:T(8,128)(2,1)S(1)}, u32[]{:S(2)}, u32[]{:S(2)}) collective-permute-start(bf16[128,2,32]{0,2,1:T(8,128)(2,1)S(1)} %reshape.212), channel_id=1, source_target_pairs={{0,1},{1,0},{2,3},{3,2},{4,5},{5,4},{6,7},{7,6},{8,9},{9,8},{10,11... | collective-permute-start | bytes 49160 | tf_op jit(solution)/shard_map/ppermute | solution.py:15
  216.1 4.7 %collective-permute-start.5 = (bf16[128,2,64]{0,2,1:T(8,128)(2,1)S(1)}, bf16[128,2,64]{0,2,1:T(8,128)(2,1)S(1)}, u32[]{:S(2)}, u32[]{:S(2)}) collective-permute-start(bf16[128,2,64]{0,2,1:T(8,128)(2,1)S(1)} %maximum_select_fusion.4), channel_id=1, source_target_pairs={{0,2},{1,3},{2,0},{3,1},{4,6},{5,7},{6,4},{7,5},{8,10},{9,11},{10,... | collective-permute-start | bytes 98312 | tf_op jit(solution)/shard_map/ppermute | solution.py:15
  220.8 4.3 %collective-permute-start.6 = (bf16[128,2,128]{0,2,1:T(8,128)(2,1)S(1)}, bf16[128,2,128]{0,2,1:T(8,128)(2,1)S(1)}, u32[]{:S(2)}, u32[]{:S(2)}) collective-permute-start(bf16[128,2,128]{0,2,1:T(8,128)(2,1)S(1)} %maximum_select_fusion.3), channel_id=1, source_target_pairs={{0,4},{1,5},{2,6},{3,7},{4,0},{5,1},{6,2},{7,3},{8,12},{9,13},{10,... | collective-permute-start | bytes 196616 | tf_op jit(solution)/shard_map/ppermute | solution.py:15
  225.2 7.3 %collective-permute-start.7 = (bf16[128,2,256]{0,2,1:T(8,128)(2,1)S(1)}, bf16[128,2,256]{0,2,1:T(8,128)(2,1)S(1)}, u32[]{:S(2)}, u32[]{:S(2)}) collective-permute-start(bf16[128,2,256]{0,2,1:T(8,128)(2,1)S(1)} %maximum_select_fusion.2), channel_id=1, source_target_pairs={{0,8},{1,9},{2,10},{3,11},{4,12},{5,13},{6,14},{7,15},{8,0},{9,1},... | collective-permute-start | bytes 393224 | tf_op jit(solution)/shard_map/ppermute | solution.py:15
